TPU v7x, 32 devices: a whole 2x2x4 slice. The times are simulated.
32 devices in a mesh: seq: 2 (over core), mp: 4 (over y, x), batch: 4 (over z).
Axes of the slice: x: 2, y: 2, z: 4, core: 2. Of those that a mesh axis runs over, the one named last changes fastest.
Arguments:
- queries: bfloat16 [4, 8, 4096], P('batch', 'seq', 'mp'), may hold values from -6 to 6
- keys: bfloat16 [4, 512, 1024], P('batch', 'seq', 'mp'), may hold values from -6 to 6
- values: bfloat16 [4, 512, 1024], P('batch', 'seq', 'mp'), may hold values from -6 to 6
- key_position: float32 [32, 128], replicated, may hold values from -4 to 4
- compress_keys: bfloat16 [4096, 128], replicated, may hold values from -0.2 to 0.2
- compress_values: bfloat16 [4096, 128], replicated, may hold values from -0.09375 to 0.09375
- out_proj: bfloat16 [4096, 4096], P('mp', 'seq'), may hold values from -0.09375 to 0.09375
- residual: bfloat16 [4, 8, 4096], P(None, None, 'seq'), may hold values from -6 to 6
- norm_gain: float32 [4096], replicated, may hold values from 0.25 to 1.75
- lm_head: bfloat16 [8192, 4096], P(('seq', 'mp', 'batch')), may hold values from -0.4 to 0.4
- targets: int32 [4, 8], replicated, may hold values from 0 to 8191
- lengths: int32 [4], replicated, may hold values from 128 to 512
Outputs:
- token_logprob: float32 [4, 8], P('batch', 'seq')
- rollout_score: float32 [4], P('batch')
All inputs are finite; a program needn't handle non-finite values.
Results may differ from a plain program's by a relative error of at most 0.0005.
The roundings to bfloat16 on the way count: a program that leaves them out, or rounds other values in their place, can miss the bound.
Values may be sent and summed in bfloat16 or wider, within the bound.
No kernel may reach another device: no remote copies, remote signals or barrier semaphores. Data moves between devices by JAX's collectives and lax.ppermute only.
A program may use at most 64 MiB of HBM per device.

v0:
```python
import math
import jax
import jax.numpy as jnp
from jax import lax
from jax.sharding import PartitionSpec as P

HEAD_DIM = 128
BLOCK = 32
STRIDE = 16


def from_behind(block, axis, distance):
    devices = range(lax.axis_size(axis))
    route = [(i - distance, i) for i in devices if i - distance in devices]
    return lax.ppermute(block, axis, route)


def compress_rows(rows, following, position, weight):
    extended = jnp.concatenate([rows, following], 0)
    count = rows.shape[0] // STRIDE
    heads = rows.shape[1] // HEAD_DIM
    shaped = extended.reshape(count + 1, STRIDE, heads, HEAD_DIM)
    blocks = jnp.concatenate([shaped[:-1], shaped[1:]], 1)
    blocks = (blocks.astype(jnp.float32) + position[None, :, None, :]).astype(jnp.bfloat16)
    mapped = jnp.einsum(
        "bjhd,jde->bhe",
        blocks,
        weight.reshape(BLOCK, HEAD_DIM, HEAD_DIM),
        preferred_element_type=jnp.float32,
    )
    return mapped.astype(jnp.bfloat16).reshape(count, heads * HEAD_DIM)


def normalize(hidden, gain):
    widened = hidden.astype(jnp.float32)
    meansq = jnp.mean(widened * widened, -1, keepdims=True)
    return (widened * lax.rsqrt(meansq + 1e-05) * gain).astype(jnp.bfloat16)


def vocab_logits(normed, rows):
    return lax.dot_general(
        normed, rows, (((1,), (1,)), ((), ())), preferred_element_type=jnp.float32
    )


def picked_logit(logits, offset, wanted):
    columns = offset + jnp.arange(logits.shape[1], dtype=jnp.int32)
    hits = columns[None, :] == wanted[:, None]
    return jnp.sum(jnp.where(hits, logits, 0.0), 1)


def body(
    queries,
    keys,
    values,
    key_position,
    compress_keys,
    compress_values,
    out_proj,
    residual,
    norm_gain,
    lm_head,
    targets,
    lengths,
):
    seq_count = lax.axis_size("seq")
    seq_pos = lax.axis_index("seq")
    batch_count = lax.axis_size("batch")
    batch_pos = lax.axis_index("batch")
    qcount = queries.shape[1]
    skip = keys.shape[1] // qcount
    scored = targets.shape[1]
    following = from_behind((keys[0, :STRIDE], values[0, :STRIDE]), "seq", -1)
    comp_keys = compress_rows(keys[0], following[0], key_position, compress_keys)
    comp_values = compress_rows(values[0], following[1], key_position, compress_values)
    every = lax.all_gather(jnp.stack([comp_keys, comp_values], 0), "seq", axis=1, tiled=True)
    heads = keys.shape[2] // HEAD_DIM
    blocks = every.shape[1]
    all_keys = every[0].reshape(blocks, heads, HEAD_DIM)
    all_values = every[1].reshape(blocks, heads, HEAD_DIM)
    group = queries.shape[2] // HEAD_DIM // heads
    query = queries[0].reshape(qcount, heads, group, HEAD_DIM)
    scores = jnp.einsum("qhgd,bhd->qhgb", query, all_keys, preferred_element_type=jnp.float32) * (
        1.0 / math.sqrt(HEAD_DIM)
    )
    index = seq_pos * qcount + jnp.arange(qcount, dtype=jnp.int32)
    limit = index * skip // STRIDE
    visible = (jnp.arange(blocks, dtype=jnp.int32)[None, :] <= limit[:, None])[:, None, None, :]
    scores = jnp.where(visible, scores, -1e30)
    peak = jnp.max(scores, -1, keepdims=True)
    weights = jnp.where(visible, jnp.exp(scores - peak), 0.0)
    probs = (weights / jnp.sum(weights, -1, keepdims=True)).astype(jnp.bfloat16)
    attended = jnp.einsum("qhgb,bhd->qhgd", probs, all_values, preferred_element_type=jnp.float32)
    attended = attended.astype(jnp.bfloat16).reshape(qcount, heads * group * HEAD_DIM)
    spots = jnp.arange(scored, dtype=jnp.int32) * skip + BLOCK - 1
    valid = (spots[None, :] < lengths[:, None]).astype(jnp.float32)
    count = jnp.sum(valid)
    width = out_proj.shape[1]
    rows_all = lax.all_gather(attended, ("seq", "batch"), axis=0, tiled=True)
    part = jnp.dot(rows_all, out_proj, preferred_element_type=jnp.float32)
    summed = lax.psum(part, "mp")
    local_res = (
        residual.reshape(batch_count, seq_count, qcount, width)
        .transpose(1, 0, 2, 3)
        .reshape(-1, width)
    )
    hidden = (local_res.astype(jnp.float32) + summed).astype(jnp.bfloat16)
    whole = lax.all_gather(hidden, "seq", axis=1, tiled=True)
    normed = normalize(whole, norm_gain)
    logits = vocab_logits(normed, lm_head)
    wanted = targets.reshape(batch_count, seq_count, qcount).transpose(1, 0, 2).reshape(-1)
    offset = lax.axis_index(("seq", "mp", "batch")) * lm_head.shape[0]
    picked = picked_logit(logits, offset, wanted)
    local_top = jnp.max(logits, 1)
    top = lax.pmax(local_top, ("seq", "mp", "batch"))
    local_sum = jnp.sum(jnp.exp(logits - top[:, None]), 1)
    total, target_logit = lax.psum((local_sum, picked), ("seq", "mp", "batch"))
    logprob = target_logit - (top + jnp.log(total))
    cube = logprob.reshape(seq_count, batch_count, qcount)
    token_logprob = cube[seq_pos, batch_pos][None, :]
    by_rollout = cube.transpose(1, 0, 2).reshape(batch_count, scored)
    sums = jnp.sum(valid * by_rollout, 1) / count
    rollout_score = sums[batch_pos][None]
    return (token_logprob, rollout_score)


def solution(mesh):
    in_specs = (
        P("batch", "seq", "mp"),
        P("batch", "seq", "mp"),
        P("batch", "seq", "mp"),
        P(),
        P(),
        P(),
        P("mp", "seq"),
        P(None, None, "seq"),
        P(),
        P(("seq", "mp", "batch"), None),
        P(),
        P(),
    )
    out_specs = (P("batch", "seq"), P("batch"))
    return jax.shard_map(body, mesh=mesh, in_specs=in_specs, out_specs=out_specs, check_vma=False)
```

profile of v0, /device:TPU:0, one launch (start us, length us, event | category | flops | bytes accessed | tf_op | source)
XLA Modules:
  0.0 194.4 jit_solution(1485913314387452292)
XLA Ops:
  7.2 0.0 copy-start
  7.2 0.0 copy-start.1
  7.2 0.0 all-reduce.3.cloned.1.call-start
  7.2 0.9 slice_bitcast_fusion.1
  8.1 1.4 collective-permute-start
  9.5 1.3 slice_bitcast_fusion
  10.8 1.3 collective-permute-start.1
  12.1 0.6 iota_compare_fusion
  12.7 0.6 multiply_add_fusion
  13.3 0.9 slice.32
  14.3 0.9 slice.36
  15.2 0.7 copy.47
  15.9 0.1 copy.50
  16.0 1.3 reshape_squeeze.11
  17.3 0.0 collective-permute-done
  17.3 0.9 pad_maximum_fusion.1
  18.2 0.1 copy.48
  18.3 1.6 fusion.6
  19.9 0.0 collective-permute-done.1
  19.9 0.9 pad_maximum_fusion
  20.9 0.0 copy-start.2
  20.9 0.1 copy.51
  21.0 0.0 copy-done.1
  21.0 0.0 copy-start.4
  21.0 0.0 copy-start.6
  21.0 1.0 fusion.7
  22.0 0.0 copy-start.3
  22.1 2.6 %all_gather.9 = bf16[2,32,256]{2,1,0:T(8,128)(2,1)S(1)} all-gather(bf16[2,16,256]{2,1,0:T(8,128)(2,1)S(1)} %pad_maximum_fusion.2), channel_id=1, replica_groups=mesh['seq'=2,'mp'=4,'batch'=4] {'seq'}, dimensions={1}, use_global_device_ids=true | all-gather | bytes 49152 | tf_op jit(solution)/shard_map/all_gather | solution.py:76
  24.7 0.8 fusion.5
  25.5 0.8 fusion.32
  26.4 0.9 fusion.8
  27.3 25.7 %all-gather = bf16[8,4,1024]{2,1,0:T(4,128)(2,1)S(1)} all-gather(bf16[1,4,1024]{2,1,0:T(4,128)(2,1)S(1)} %reshape.113), channel_id=1, replica_groups=mesh['seq'=2,'mp'=4,'batch'=4] {'seq','batch'}, dimensions={0}, use_global_device_ids=true | all-gather | bytes 73728 | tf_op jit(solution)/shard_map/all_gather | solution.py:99
  53.0 0.0 copy-start.5
  53.0 3.7 %fusion.34 = f32[32,2048]{1,0:T(8,128)} fusion(bf16[32,1024]{1,0:T(8,128)(2,1)S(1)} %reshape.114, bf16[1024,2048]{1,0:T(8,128)(2,1)} %param.18), kind=kOutput, calls=%fused_computation.65 | convolution fusion | flops 134217728 | bytes 4521984 | tf_op jit(solution)/shard_map/dot_general | solution.py:100
  56.7 0.0 all-reduce.3.cloned.1.call-update
  56.8 0.0 copy-done.2
  56.8 0.1 reshape.112
  56.9 0.1 reshape.111
  57.0 0.0 copy-done.4
  57.0 0.1 reshape.106
  57.1 0.1 eq.16
  57.2 0.0 copy-done.6
  57.2 0.7 convert_reduce_fusion
  57.9 43.1 %all-reduce.3.cloned.1.call-done = f32[32,2048]{1,0:T(8,128)} async-done(((f32[32,2048]{1,0:T(8,128)}), f32[32,2048]{1,0:T(8,128)}) %all-reduce.3.cloned.1.call-update) | async-done | bytes 262160 | tf_op jit(solution)/shard_map/psum | solution.py:101
  101.0 1.0 add_convert_fusion.4
  102.0 2.0 %all_gather.11 = bf16[32,4096]{1,0:T(8,128)(2,1)S(1)} all-gather(bf16[32,2048]{1,0:T(8,128)(2,1)S(1)} %add_convert_fusion.4), channel_id=1, replica_groups=mesh['seq'=2,'mp'=4,'batch'=4] {'seq'}, dimensions={1}, use_global_device_ids=true | all-gather | bytes 393216 | tf_op jit(solution)/shard_map/all_gather | solution.py:108
  104.0 0.2 fusion.9
  104.1 0.0 copy-done
  104.1 0.0 copy-done.3
  104.2 0.8 fusion.33
  105.0 39.3 %pmax.7 = f32[32]{0:T(128)S(1)} all-reduce(f32[32]{0:T(128)S(1)} %get-tuple-element.8), channel_id=1, replica_groups=mesh['seq'=2,'mp'=4,'batch'=4] {'seq','mp','batch'}, use_global_device_ids=true, to_apply=%region_7.8 | all-reduce | flops 32 | bytes 256 | tf_op jit(solution)/shard_map/pmax | solution.py:115
  144.3 0.2 exponential_reduce_fusion
  144.5 41.0 %all-reduce = (f32[32]{0:T(128)S(1)}, f32[32]{0:T(128)S(1)}) all-reduce(f32[32]{0:T(128)S(1)} %get-tuple-element.3, f32[32]{0:T(128)S(1)} %get-tuple-element.2), channel_id=1, replica_groups=mesh['seq'=2,'mp'=4,'batch'=4] {'seq','mp','batch'}, use_global_device_ids=true, to_apply=%region_5.6 | all-reduce | flops 64 | bytes 512 | tf_op jit(solution)/shard_map/psum | solution.py:117
  185.5 0.1 reshape.110
  185.6 0.0 copy-done.5
  185.6 0.2 fusion.28
  185.8 0.7 broadcast_divide_fusion
  186.4 0.6 dynamic_slice.7
  187.0 0.5 dynamic-slice_bitcast_fusion
  (20 shorter events, 0.2 us)
Async XLA Ops:
  7.2 97.0 %copy-start = (bf16[256,4096]{1,0:T(8,128)(2,1)S(1)}, bf16[256,4096]{1,0:T(8,128)(2,1)}, u32[]{:S(2)}) copy-start(bf16[256,4096]{1,0:T(8,128)(2,1)} %param.21) | copy-start | bytes 6291460
  7.2 13.8 %copy-start.1 = (bf16[4096,128]{1,0:T(8,128)(2,1)S(1)}, bf16[4096,128]{1,0:T(8,128)(2,1)}, u32[]{:S(2)}) copy-start(bf16[4096,128]{1,0:T(8,128)(2,1)} %param.17) | copy-start | bytes 3145732
  7.2 93.8 %all-reduce.3.cloned.1.call-start = ((), (), s32[]{:S(2)}) async-start(), calls=%async_computation | async-start | bytes 524288 | tf_op jit(solution)/shard_map/psum | solution.py:101
  8.1 9.1 %collective-permute-start = (bf16[16,256]{1,0:T(8,128)(2,1)S(1)}, bf16[16,256]{1,0:T(8,128)(2,1)S(1)}, u32[]{:S(2)}, u32[]{:S(2)}) collective-permute-start(bf16[16,256]{1,0:T(8,128)(2,1)S(1)} %slice_bitcast_fusion.1), channel_id=1, source_target_pairs={{16,0},{17,1},{18,2},{19,3},{20,4},{21,5},{22,6},{23,7},{24,8},{25... | collective-permute-start | bytes 24584 | tf_op jit(solution)/shard_map/ppermute | solution.py:15
  10.8 9.1 %collective-permute-start.1 = (bf16[16,256]{1,0:T(8,128)(2,1)}, bf16[16,256]{1,0:T(8,128)(2,1)S(1)}, u32[]{:S(2)}, u32[]{:S(2)}) collective-permute-start(bf16[16,256]{1,0:T(8,128)(2,1)} %slice_bitcast_fusion), channel_id=1, source_target_pairs={{16,0},{17,1},{18,2},{19,3},{20,4},{21,5},{22,6},{23,7},{24,8},{25... | collective-permute-start | bytes 24584 | tf_op jit(solution)/shard_map/ppermute | solution.py:15
  20.9 35.9 %copy-start.2 = (bf16[4,8,2048]{2,1,0:T(8,128)(2,1)S(1)}, bf16[4,8,2048]{2,1,0:T(8,128)(2,1)}, u32[]{:S(2)}) copy-start(bf16[4,8,2048]{2,1,0:T(8,128)(2,1)} %param.19) | copy-start | bytes 393220
  21.0 36.0 %copy-start.4 = (s32[4,8]{1,0:T(4,128)S(1)}, s32[4,8]{1,0:T(4,128)}, u32[]{:S(2)}) copy-start(s32[4,8]{1,0:T(4,128)} %param.22) | copy-start | bytes 388
  21.0 36.2 %copy-start.6 = (s32[4]{0:T(128)S(1)}, s32[4]{0:T(128)}, u32[]{:S(2)}) copy-start(s32[4]{0:T(128)} %param.23) | copy-start | bytes 52
  22.0 82.1 %copy-start.3 = (f32[4096]{0:T(1024)S(1)}, f32[4096]{0:T(1024)}, u32[]{:S(2)}) copy-start(f32[4096]{0:T(1024)} %param.20) | copy-start | bytes 49156
  53.0 132.6 %copy-start.5 = (s32[2,4]{1,0:T(2,128)S(1)}, s32[2,4]{1,0:T(2,128)}, u32[]{:S(2)}) copy-start(s32[2,4]{1,0:T(2,128)} %multiply_add_fusion) | copy-start | bytes 100
Sparse Core Ops, SparseCore 0:
  56.9 44.0 all-reduce.2
where the time goes:
time: 195 us; the launch traced here: 194 us
  blocking collectives  111 us (57%)
  waiting for transfers between devices  43.1 us (22%)
  between operations  14.3 us (7%)
  matrix products  8.86 us (5%)
  local copies, waits for them, and re-layouts  8.01 us (4%)
  other arithmetic  6.72 us (3%)
  starting transfers between devices  2.73 us (1%)
    psum x1, waiting for transfers between devices, body(): summed = lax.psum(part, 'mp')  43.1 us
    psum x1, blocking collectives, body(): total, target_logit = lax.psum((local_sum, picked), ('seq', 'mp', 'batch'))  41 us
    pmax x1, blocking collectives, body(): top = lax.pmax(local_top, ('seq', 'mp', 'batch'))  39.3 us
    all_gather x1, blocking collectives, body(): rows_all = lax.all_gather(attended, ('seq', 'batch'), axis=0, tiled=True)  25.7 us
  transfers between devices with their start and end apart: 3, of which 1 were waited for; matrix products, arithmetic and copies ran while one was open for 5% of the time, Pallas kernels for 0%

commit v1 on v0

--- a/solution.py
+++ b/solution.py
@@ -96,7 +96,33 @@
     valid = (spots[None, :] < lengths[:, None]).astype(jnp.float32)
     count = jnp.sum(valid)
     width = out_proj.shape[1]
-    rows_all = lax.all_gather(attended, ("seq", "batch"), axis=0, tiled=True)
+    bank = []
+    wide_out, u_next, last = (
+        jax.lax.axis_size(("seq", "batch")),
+        jax.lax.axis_index(("seq", "batch")),
+        attended.shape[0],
+    )
+    for kk in range(wide_out):
+        bank.append((kk, (kk + 1) % wide_out))
+    frames = []
+    for kk in range(wide_out):
+        frames.append((kk, (kk - 1) % wide_out))
+    rows_all = jnp.zeros(
+        (*attended.shape[:0], wide_out * last, *attended.shape[1:]), attended.dtype
+    )
+    rows_all = lax.dynamic_update_slice_in_dim(rows_all, attended, u_next * last, axis=0)
+    vec_out = m_next = attended
+    local_part = wide_out // 2
+    for p in range(1, local_part + 1):
+        vec_out = jax.lax.ppermute(vec_out, ("seq", "batch"), bank)
+        rows_all = lax.dynamic_update_slice_in_dim(
+            rows_all, vec_out, (u_next - p) % wide_out * last, axis=0
+        )
+        if p < wide_out - local_part:
+            m_next = jax.lax.ppermute(m_next, ("seq", "batch"), perm=frames)
+            rows_all = lax.dynamic_update_slice_in_dim(
+                rows_all, m_next, (u_next + p) % wide_out * last, axis=0
+            )
     part = jnp.dot(rows_all, out_proj, preferred_element_type=jnp.float32)
     summed = lax.psum(part, "mp")
     local_res = (

time: 195 us -> 189 us (0.969)
  blocking collectives: 111 us -> 85.5 us
  starting transfers between devices: 2.73 us -> 15 us
  waiting for transfers between devices: 43.1 us -> 49 us
    all_gather x1 -> x0, blocking collectives: 25.7 us -> none  [body(): rows_all = lax.all_gather(attended, ('seq', 'batch'), axis=0, tiled=True)]
    ppermute x0 -> x7, starting transfers between devices: none -> 12.3 us  [the longest x3 8.86 us: body(): m_next = jax.lax.ppermute(m_next, ('seq', 'batch'), perm=frames)]
    ppermute x0 -> x7, waiting for transfers between devices: none -> 8.62 us  [the longest x4 8.36 us: body(): vec_out = jax.lax.ppermute(vec_out, ('seq', 'batch'), bank)]
    psum x1, waiting for transfers between devices: 43.1 us -> 40.3 us  [body(): summed = lax.psum(part, 'mp')]
  transfers between devices with their start and end apart: 3 -> 10, of which waited for: 1 -> 7; matrix products, arithmetic and copies ran while one was open for 5% -> 6% of each run, Pallas kernels for 0% -> 0%
where the time goes in v1:
time: 189 us; the launch traced here: 188 us
  blocking collectives  85.5 us (45%)
  waiting for transfers between devices  49 us (26%)
  starting transfers between devices  15 us (8%)
  between operations  14.4 us (8%)
  local copies, waits for them, and re-layouts  8.67 us (5%)
  matrix products  8.13 us (4%)
  other arithmetic  7.43 us (4%)
    psum x1, blocking collectives, body(): total, target_logit = lax.psum((local_sum, picked), ('seq', 'mp', 'batch'))  41 us
    psum x1, waiting for transfers between devices, body(): summed = lax.psum(part, 'mp')  40.3 us
    pmax x1, blocking collectives, body(): top = lax.pmax(local_top, ('seq', 'mp', 'batch'))  39.3 us
    ppermute x3, starting transfers between devices, body(): m_next = jax.lax.ppermute(m_next, ('seq', 'batch'), perm=frames)  8.86 us
    ppermute x4, waiting for transfers between devices, body(): vec_out = jax.lax.ppermute(vec_out, ('seq', 'batch'), bank)  8.36 us
  transfers between devices with their start and end apart: 10, of which 7 were waited for; matrix products, arithmetic and copies ran while one was open for 6% of the time, Pallas kernels for 0%

profile of v1, /device:TPU:0, one launch (start us, length us, event | category | flops | bytes accessed | tf_op | source)
XLA Modules:
  0.0 188.2 jit_solution(7337722167977617505)
XLA Ops:
  7.2 0.0 copy-start
  7.2 0.0 copy-start.2
  7.2 0.0 all-reduce.3.cloned.1.call-start
  7.2 0.9 slice_bitcast_fusion.1
  8.1 1.4 collective-permute-start
  9.5 1.3 slice_bitcast_fusion
  10.8 1.3 collective-permute-start.1
  12.1 0.6 iota_compare_fusion
  12.7 0.6 multiply_add_fusion
  13.3 0.9 slice.32
  14.2 0.9 slice.36
  15.3 0.7 copy.35
  16.0 0.1 copy.38
  16.0 1.3 reshape_squeeze.11
  17.3 0.0 collective-permute-done
  17.3 0.9 pad_maximum_fusion.1
  18.3 0.1 copy.36
  18.4 1.6 fusion.6
  20.0 0.6 stack_reshape.6
  20.6 0.0 collective-permute-done.1
  20.6 0.9 pad_maximum_fusion
  21.6 0.0 copy-start.3
  21.6 0.1 copy.39
  21.6 0.0 copy-start.5
  21.7 0.0 copy-start.7
  21.7 0.3 fusion.7
  22.0 0.0 copy-start.4
  22.0 0.7 pad_maximum_fusion.2
  22.7 3.2 %all_gather.6 = bf16[2,32,256]{2,1,0:T(8,128)(2,1)S(1)} all-gather(bf16[2,16,256]{2,1,0:T(8,128)(2,1)S(1)} %pad_maximum_fusion.2), channel_id=1, replica_groups=mesh['seq'=2,'mp'=4,'batch'=4] {'seq'}, dimensions={1}, use_global_device_ids=true | all-gather | bytes 49152 | tf_op jit(solution)/shard_map/all_gather | solution.py:76
  25.9 0.8 fusion.5
  26.7 0.8 fusion.33
  27.6 0.9 fusion.8
  28.5 3.1 %collective-permute-start.2 = (bf16[4,1024]{1,0:T(4,128)(2,1)S(1)}, bf16[4,1024]{1,0:T(4,128)(2,1)S(1)}, u32[]{:S(2)}, u32[]{:S(2)}) collective-permute-start(bf16[4,1024]{1,0:T(4,128)(2,1)S(1)} %reshape.109), channel_id=1, source_target_pairs={{0,1},{1,2},{2,3},{3,16},{16,17},{17,18},{18,19},{19,0},{4,5},{5,6... | collective-permute-start | bytes 24584 | tf_op jit(solution)/shard_map/ppermute | solution.py:117
  31.6 2.0 %collective-permute-start.3 = (bf16[4,1024]{1,0:T(4,128)(2,1)S(1)}, bf16[4,1024]{1,0:T(4,128)(2,1)S(1)}, u32[]{:S(2)}, u32[]{:S(2)}) collective-permute-start(bf16[4,1024]{1,0:T(4,128)(2,1)S(1)} %reshape.109), channel_id=1, source_target_pairs={{0,19},{1,0},{2,1},{3,2},{16,3},{17,16},{18,17},{19,18},{4,23},{5,... | collective-permute-start | bytes 24584 | tf_op jit(solution)/shard_map/ppermute | solution.py:122
  33.7 1.2 collective-permute-done.2
  34.9 0.3 collective-permute-start.4
  35.2 0.0 collective-permute-done.3
  35.3 3.3 %collective-permute-start.5 = (bf16[4,1024]{1,0:T(4,128)(2,1)S(1)}, bf16[4,1024]{1,0:T(4,128)(2,1)S(1)}, u32[]{:S(2)}, u32[]{:S(2)}) collective-permute-start(bf16[4,1024]{1,0:T(4,128)(2,1)S(1)} %collective-permute-done.3), channel_id=1, source_target_pairs={{0,19},{1,0},{2,1},{3,2},{16,3},{17,16},{18,17},{19,18},{4,23},{5,... | collective-permute-start | bytes 24584 | tf_op jit(solution)/shard_map/ppermute | solution.py:122
  38.6 1.2 collective-permute-done.4
  39.8 0.1 collective-permute-done.5
  39.9 3.5 %collective-permute-start.7 = (bf16[4,1024]{1,0:T(4,128)(2,1)S(1)}, bf16[4,1024]{1,0:T(4,128)(2,1)S(1)}, u32[]{:S(2)}, u32[]{:S(2)}) collective-permute-start(bf16[4,1024]{1,0:T(4,128)(2,1)S(1)} %collective-permute-done.5), channel_id=1, source_target_pairs={{0,19},{1,0},{2,1},{3,2},{16,3},{17,16},{18,17},{19,18},{4,23},{5,... | collective-permute-start | bytes 24584 | tf_op jit(solution)/shard_map/ppermute | solution.py:122
  43.5 1.2 collective-permute-done.6
  44.7 0.1 collective-permute-done.7
  44.8 4.7 %collective-permute-done.8 = bf16[4,1024]{1,0:T(4,128)(2,1)S(1)} collective-permute-done((bf16[4,1024]{1,0:T(4,128)(2,1)S(1)}, bf16[4,1024]{1,0:T(4,128)(2,1)S(1)}, u32[]{:S(2)}, u32[]{:S(2)}) %collective-permute-start.8) | collective-permute-done | bytes 8224 | tf_op jit(solution)/shard_map/ppermute | solution.py:117
  49.6 3.7 %fusion.35 = f32[32,2048]{1,0:T(8,128)} fusion(bf16[32,1024]{1,0:T(8,128)(2,1)S(1)} %constant_dynamic-update-slice_fusion, bf16[1024,2048]{1,0:T(8,128)(2,1)} %param.18), kind=kOutput, calls=%fused_computation.74 | convolution fusion | flops 134217728 | bytes 4521984 | tf_op jit(solution)/shard_map/dot_general | solution.py:126
  53.3 0.0 all-reduce.3.cloned.1.call-update
  53.3 0.1 reshape.112
  53.4 0.1 reshape.111
  53.6 0.1 reshape.106
  53.6 0.1 eq.24
  53.7 0.7 convert_reduce_fusion
  54.4 40.3 %all-reduce.3.cloned.1.call-done = f32[32,2048]{1,0:T(8,128)} async-done(((f32[32,2048]{1,0:T(8,128)}), f32[32,2048]{1,0:T(8,128)}) %all-reduce.3.cloned.1.call-update) | async-done | bytes 262160 | tf_op jit(solution)/shard_map/psum | solution.py:127
  94.8 1.0 add_convert_fusion.4
  95.7 2.0 %all_gather.7 = bf16[32,4096]{1,0:T(8,128)(2,1)S(1)} all-gather(bf16[32,2048]{1,0:T(8,128)(2,1)S(1)} %add_convert_fusion.4), channel_id=1, replica_groups=mesh['seq'=2,'mp'=4,'batch'=4] {'seq'}, dimensions={1}, use_global_device_ids=true | all-gather | bytes 393216 | tf_op jit(solution)/shard_map/all_gather | solution.py:134
  97.7 0.2 fusion.9
  97.9 0.8 fusion.34
  98.8 39.3 %pmax.7 = f32[32]{0:T(128)S(1)} all-reduce(f32[32]{0:T(128)S(1)} %get-tuple-element.8), channel_id=1, replica_groups=mesh['seq'=2,'mp'=4,'batch'=4] {'seq','mp','batch'}, use_global_device_ids=true, to_apply=%region_7.8 | all-reduce | flops 32 | bytes 256 | tf_op jit(solution)/shard_map/pmax | solution.py:141
  138.1 0.2 exponential_reduce_fusion
  138.3 41.0 %all-reduce = (f32[32]{0:T(128)S(1)}, f32[32]{0:T(128)S(1)}) all-reduce(f32[32]{0:T(128)S(1)} %get-tuple-element.3, f32[32]{0:T(128)S(1)} %get-tuple-element.2), channel_id=1, replica_groups=mesh['seq'=2,'mp'=4,'batch'=4] {'seq','mp','batch'}, use_global_device_ids=true, to_apply=%region_5.6 | all-reduce | flops 64 | bytes 512 | tf_op jit(solution)/shard_map/psum | solution.py:143
  179.3 0.1 reshape.110
  179.4 0.2 fusion.28
  179.5 0.7 broadcast_divide_fusion
  180.2 0.6 dynamic_slice.7
  180.8 0.5 fusion.29
  (38 shorter events, 0.3 us)
Async XLA Ops:
  7.2 90.8 %copy-start = (bf16[256,4096]{1,0:T(8,128)(2,1)S(1)}, bf16[256,4096]{1,0:T(8,128)(2,1)}, u32[]{:S(2)}) copy-start(bf16[256,4096]{1,0:T(8,128)(2,1)} %param.21) | copy-start | bytes 6291460
  7.2 14.5 %copy-start.2 = (f32[32,128]{1,0:T(8,128)S(1)}, f32[32,128]{1,0:T(8,128)}, u32[]{:S(2)}) copy-start(f32[32,128]{1,0:T(8,128)} %param.15) | copy-start | bytes 49156
  7.2 14.5 %copy-start.1 = (bf16[4096,128]{1,0:T(8,128)(2,1)S(1)}, bf16[4096,128]{1,0:T(8,128)(2,1)}, u32[]{:S(2)}) copy-start(bf16[4096,128]{1,0:T(8,128)(2,1)} %param.17) | copy-start | bytes 3145732
  7.2 87.6 %all-reduce.3.cloned.1.call-start = ((), (), s32[]{:S(2)}) async-start(), calls=%async_computation | async-start | bytes 524288 | tf_op jit(solution)/shard_map/psum | solution.py:127
  8.1 9.2 %collective-permute-start = (bf16[16,256]{1,0:T(8,128)(2,1)S(1)}, bf16[16,256]{1,0:T(8,128)(2,1)S(1)}, u32[]{:S(2)}, u32[]{:S(2)}) collective-permute-start(bf16[16,256]{1,0:T(8,128)(2,1)S(1)} %slice_bitcast_fusion.1), channel_id=1, source_target_pairs={{16,0},{17,1},{18,2},{19,3},{20,4},{21,5},{22,6},{23,7},{24,8},{25... | collective-permute-start | bytes 24584 | tf_op jit(solution)/shard_map/ppermute | solution.py:15
  10.8 9.8 %collective-permute-start.1 = (bf16[16,256]{1,0:T(8,128)(2,1)}, bf16[16,256]{1,0:T(8,128)(2,1)}, u32[]{:S(2)}, u32[]{:S(2)}) collective-permute-start(bf16[16,256]{1,0:T(8,128)(2,1)} %slice_bitcast_fusion), channel_id=1, source_target_pairs={{16,0},{17,1},{18,2},{19,3},{20,4},{21,5},{22,6},{23,7},{24,8},{25... | collective-permute-start | bytes 24584 | tf_op jit(solution)/shard_map/ppermute | solution.py:15
  21.6 31.7 %copy-start.3 = (bf16[4,8,2048]{2,1,0:T(8,128)(2,1)S(1)}, bf16[4,8,2048]{2,1,0:T(8,128)(2,1)}, u32[]{:S(2)}) copy-start(bf16[4,8,2048]{2,1,0:T(8,128)(2,1)} %param.19) | copy-start | bytes 393220
  21.6 31.9 %copy-start.5 = (s32[4,8]{1,0:T(4,128)S(1)}, s32[4,8]{1,0:T(4,128)}, u32[]{:S(2)}) copy-start(s32[4,8]{1,0:T(4,128)} %param.22) | copy-start | bytes 388
  21.7 32.1 %copy-start.7 = (s32[4]{0:T(128)S(1)}, s32[4]{0:T(128)}, u32[]{:S(2)}) copy-start(s32[4]{0:T(128)} %param.23) | copy-start | bytes 52
  22.0 76.0 %copy-start.4 = (f32[4096]{0:T(1024)S(1)}, f32[4096]{0:T(1024)}, u32[]{:S(2)}) copy-start(f32[4096]{0:T(1024)} %param.20) | copy-start | bytes 49156
  28.5 6.4 %collective-permute-start.2 = (bf16[4,1024]{1,0:T(4,128)(2,1)S(1)}, bf16[4,1024]{1,0:T(4,128)(2,1)S(1)}, u32[]{:S(2)}, u32[]{:S(2)}) collective-permute-start(bf16[4,1024]{1,0:T(4,128)(2,1)S(1)} %reshape.109), channel_id=1, source_target_pairs={{0,1},{1,2},{2,3},{3,16},{16,17},{17,18},{18,19},{19,0},{4,5},{5,6... | collective-permute-start | bytes 24584 | tf_op jit(solution)/shard_map/ppermute | solution.py:117
  31.6 3.7 %collective-permute-start.3 = (bf16[4,1024]{1,0:T(4,128)(2,1)S(1)}, bf16[4,1024]{1,0:T(4,128)(2,1)S(1)}, u32[]{:S(2)}, u32[]{:S(2)}) collective-permute-start(bf16[4,1024]{1,0:T(4,128)(2,1)S(1)} %reshape.109), channel_id=1, source_target_pairs={{0,19},{1,0},{2,1},{3,2},{16,3},{17,16},{18,17},{19,18},{4,23},{5,... | collective-permute-start | bytes 24584 | tf_op jit(solution)/shard_map/ppermute | solution.py:122
  34.9 4.9 %collective-permute-start.4 = (bf16[4,1024]{1,0:T(4,128)(2,1)S(1)}, bf16[4,1024]{1,0:T(4,128)(2,1)S(1)}, u32[]{:S(2)}, u32[]{:S(2)}) collective-permute-start(bf16[4,1024]{1,0:T(4,128)(2,1)S(1)} %collective-permute-done.2), channel_id=1, source_target_pairs={{0,1},{1,2},{2,3},{3,16},{16,17},{17,18},{18,19},{19,0},{4,5},{5,6... | collective-permute-start | bytes 24584 | tf_op jit(solution)/shard_map/ppermute | solution.py:117
  35.3 4.7 %collective-permute-start.5 = (bf16[4,1024]{1,0:T(4,128)(2,1)S(1)}, bf16[4,1024]{1,0:T(4,128)(2,1)S(1)}, u32[]{:S(2)}, u32[]{:S(2)}) collective-permute-start(bf16[4,1024]{1,0:T(4,128)(2,1)S(1)} %collective-permute-done.3), channel_id=1, source_target_pairs={{0,19},{1,0},{2,1},{3,2},{16,3},{17,16},{18,17},{19,18},{4,23},{5,... | collective-permute-start | bytes 24584 | tf_op jit(solution)/shard_map/ppermute | solution.py:122
  39.8 4.9 %collective-permute-start.6 = (bf16[4,1024]{1,0:T(4,128)(2,1)S(1)}, bf16[4,1024]{1,0:T(4,128)(2,1)S(1)}, u32[]{:S(2)}, u32[]{:S(2)}) collective-permute-start(bf16[4,1024]{1,0:T(4,128)(2,1)S(1)} %collective-permute-done.4), channel_id=1, source_target_pairs={{0,1},{1,2},{2,3},{3,16},{16,17},{17,18},{18,19},{19,0},{4,5},{5,6... | collective-permute-start | bytes 24584 | tf_op jit(solution)/shard_map/ppermute | solution.py:117
  39.9 4.9 %collective-permute-start.7 = (bf16[4,1024]{1,0:T(4,128)(2,1)S(1)}, bf16[4,1024]{1,0:T(4,128)(2,1)S(1)}, u32[]{:S(2)}, u32[]{:S(2)}) collective-permute-start(bf16[4,1024]{1,0:T(4,128)(2,1)S(1)} %collective-permute-done.5), channel_id=1, source_target_pairs={{0,19},{1,0},{2,1},{3,2},{16,3},{17,16},{18,17},{19,18},{4,23},{5,... | collective-permute-start | bytes 24584 | tf_op jit(solution)/shard_map/ppermute | solution.py:122
  44.7 4.9 %collective-permute-start.8 = (bf16[4,1024]{1,0:T(4,128)(2,1)S(1)}, bf16[4,1024]{1,0:T(4,128)(2,1)S(1)}, u32[]{:S(2)}, u32[]{:S(2)}) collective-permute-start(bf16[4,1024]{1,0:T(4,128)(2,1)S(1)} %collective-permute-done.6), channel_id=1, source_target_pairs={{0,1},{1,2},{2,3},{3,16},{16,17},{17,18},{18,19},{19,0},{4,5},{5,6... | collective-permute-start | bytes 24584 | tf_op jit(solution)/shard_map/ppermute | solution.py:117
  49.5 129.8 %copy-start.6 = (s32[2,4]{1,0:T(2,128)S(1)}, s32[2,4]{1,0:T(2,128)}, u32[]{:S(2)}) copy-start(s32[2,4]{1,0:T(2,128)} %multiply_add_fusion) | copy-start | bytes 100
Sparse Core Ops, SparseCore 0:
  53.4 41.2 all-reduce.2
